TPU v7x, 64 devices: a 2x2x8 block of a 4x4x8 slice. The times are simulated.
64 devices in a mesh: dp: 4 (over x, y), ep: 16 (over z, core).
Axes of the slice: x: 2, y: 2, z: 8, core: 2. Of those that a mesh axis runs over, the one named last changes fastest.
The devices are a block of a 4x4x8 slice.
Arguments:
- x_in: bfloat16 [1536, 2048], P(('dp', 'ep')), parts along dimension 0
- topk_idx: int32 [1536, 8], P(('dp', 'ep')), parts along dimension 0
- topk_w: float32 [1536, 8], P(('dp', 'ep')), parts along dimension 0
- w_up: bfloat16 [64, 2048, 1024], P('ep')
- w_down: bfloat16 [64, 1024, 2048], P('ep')
Outputs:
- output: bfloat16 [1536, 2048], P(('dp', 'ep')), parts along dimension 0
There are 4 independent parts. A program takes and returns all parts, laid end to end along the dimension named above; an argument that names none is the same for every part.
All inputs are finite; a program needn't handle non-finite values.
Results may differ from a plain program's by a relative error of at most 0.001.
Values are sent between devices in bfloat16 or wider.
A program may use at most 768 MiB of HBM per device.

v0:
```python
import jax
import jax.numpy as jnp
from jax import lax
from jax.sharding import PartitionSpec as P


def slot_layout(expert_ids, num_experts, slot_cap):
    flat_ids = expert_ids.reshape(-1)
    expert_hits = (flat_ids[:, None] == jnp.arange(num_experts, dtype=jnp.int32)[None, :]).astype(jnp.int32)
    earlier = jnp.cumsum(expert_hits, axis=0) - expert_hits
    return flat_ids * slot_cap + jnp.sum(earlier * expert_hits, axis=1)


def solution(mesh):
    group = mesh.shape['ep']
    token_spec = P(('dp', 'ep'), None)
    expert_spec = P('ep', None, None)

    def local_layer(x_loc, ids_loc, gates_loc, w_up, w_down):
        tok_n, top_n = ids_loc.shape
        model_dim = x_loc.shape[1]
        local_experts = w_up.shape[0]
        num_experts = local_experts * group
        slot_cap = tok_n // 2
        slot_ids = slot_layout(ids_loc, num_experts, slot_cap)
        slot_range = jnp.arange(num_experts * slot_cap, dtype=jnp.int32)
        placed = jnp.any(slot_ids.reshape(tok_n, top_n, 1) == slot_range, axis=1).astype(jnp.bfloat16)
        send_rows = jnp.einsum('ts,tm->sm', placed, x_loc, preferred_element_type=jnp.float32).astype(jnp.bfloat16)
        send_rows = send_rows.reshape(group, local_experts, slot_cap, model_dim)
        recv_rows = lax.all_to_all(send_rows, 'ep', 0, 2, tiled=True)
        recv_rows = recv_rows.reshape(local_experts, group * slot_cap, model_dim)
        hidden = jnp.einsum('ecm,emf->ecf', recv_rows, w_up, preferred_element_type=jnp.float32)
        hidden = jax.nn.gelu(hidden, approximate=True).astype(jnp.bfloat16)
        expert_out = jnp.einsum('ecf,efm->ecm', hidden, w_down, preferred_element_type=jnp.float32).astype(jnp.bfloat16)
        expert_out = expert_out.reshape(1, local_experts, group * slot_cap, model_dim)
        back_rows = lax.all_to_all(expert_out, 'ep', 2, 0, tiled=True)
        back_rows = back_rows.reshape(num_experts * slot_cap, model_dim)
        picked = jnp.take(back_rows, slot_ids, axis=0).reshape(tok_n, top_n, model_dim)
        mixed = jnp.sum(gates_loc[:, :, None] * picked.astype(jnp.float32), axis=1)
        return mixed.astype(jnp.bfloat16)

    return jax.shard_map(local_layer, mesh=mesh, in_specs=(token_spec, token_spec, token_spec, expert_spec, expert_spec), out_specs=token_spec, check_vma=False)
```

profile of v0, /device:TPU:21, one launch (start us, length us, event | category | flops | bytes accessed | tf_op | source)
XLA Modules:
  0.0 205.2 jit_solution(7035957028865449591)
XLA Ops:
  0.0 0.0 copy-start
  0.0 0.8 copy.30
  0.8 0.1 reshape.79
  0.9 0.6 reduce-window.6
  1.5 0.2 slice_reduce_fusion
  1.8 0.1 bitcast_bitcast_fusion
  1.9 0.1 reduce_sum.23
  2.0 0.2 fusion.20
  2.3 0.0 copy-done
  2.3 1.0 convolution_convert_fusion
  3.3 2.7 %reshape.82 = bf16[16,4,12,2048]{3,2,1,0:T(8,128)(2,1)} reshape(bf16[768,2048]{1,0:T(8,128)(2,1)S(1)} %convolution_convert_fusion) | data formatting | bytes 6291456 | tf_op jit(solution)/shard_map/reshape | solution.py:29
  6.0 4.9 %copy.34 = bf16[16,4,12,2048]{3,1,2,0:T(4,128)(2,1)S(1)} copy(bf16[16,4,12,2048]{3,2,1,0:T(8,128)(2,1)} %reshape.82) | data formatting | bytes 6291456 | tf_op jit(solution)/shard_map/reshape | solution.py:29
  10.9 83.8 %all_to_all.30 = bf16[16,4,12,2048]{3,1,2,0:T(4,128)(2,1)S(1)} all-to-all(bf16[16,4,12,2048]{3,1,2,0:T(4,128)(2,1)S(1)} %copy.34), channel_id=1, replica_groups=mesh['dp'=4,'ep'=16] {'ep'}, dimensions={0} | all-to-all | bytes 6291456 | tf_op jit(solution)/shard_map/all_to_all | solution.py:30
  94.6 16.8 %fusion.10 = bf16[1,4,192,2048]{3,2,1,0:T(8,128)(2,1)} fusion(bf16[4,1024,2048]{2,1,0:T(8,128)(2,1)} %param.9, bf16[4,2048,1024]{2,1,0:T(8,128)(2,1)} %param.8, bf16[4,192,2048]{2,0,1:T(4,128)(2,1)S(1)} %bitcast.35), kind=kOutput, calls=%fused_computation.14 | convolution fusion | flops 6451101696 | bytes 39845888 | tf_op jit(solution)/shard_map/ecf,efm->ecm/dot_general | solution.py:34
  111.5 6.0 %copy.36 = bf16[1,4,192,2048]{3,1,0,2:T(4,128)(2,1)} copy(bf16[1,4,192,2048]{3,2,1,0:T(8,128)(2,1)} %fusion.10) | data formatting | bytes 6291456 | tf_op jit(solution)/shard_map/reshape | solution.py:35
  117.5 0.0 copy-start.1
  117.5 4.3 %all-to-all-start.1 = ((bf16[1,4,192,2048]{3,1,0,2:T(4,128)(2,1)}), bf16[1,4,192,2048]{3,1,0,2:T(4,128)(2,1)S(1)}, u32[]{:S(2)}, u32[]{:S(2)}) async-start(bf16[1,4,192,2048]{3,1,0,2:T(4,128)(2,1)} %copy.36), calls=%async_computation.1 | async-start | bytes 6291456 | tf_op jit(solution)/shard_map/all_to_all | solution.py:36
  121.7 0.1 mul.64
  121.8 0.0 copy-done.1
  121.8 0.1 copy.29
  121.9 69.3 %all-to-all-done.1 = bf16[1,4,192,2048]{3,1,0,2:T(4,128)(2,1)S(1)} async-done(((bf16[1,4,192,2048]{3,1,0,2:T(4,128)(2,1)}), bf16[1,4,192,2048]{3,1,0,2:T(4,128)(2,1)S(1)}, u32[]{:S(2)}, u32[]{:S(2)}) %all-to-all-start.1) | async-done | bytes 3145760 | tf_op jit(solution)/shard_map/all_to_all | solution.py:36
  191.2 4.2 %copy.37 = bf16[16,1,4,12,2048]{4,3,2,0,1:T(8,128)(2,1)} copy(bf16[16,1,4,12,2048]{4,2,3,0,1:T(4,128)(2,1)S(1)} %bitcast.34) | data formatting | bytes 6291456 | tf_op jit(solution)/shard_map/all_to_all | solution.py:36
  195.5 4.7 %reshape.85 = bf16[768,2048]{1,0:T(8,128)(2,1)S(1)} reshape(bf16[16,1,4,12,2048]{4,3,2,0,1:T(8,128)(2,1)} %copy.37) | data formatting | bytes 6291456 | tf_op jit(solution)/shard_map/reshape | solution.py:37
  200.2 2.0 gather_fusion
  202.2 2.9 %multiply_reduce_fusion = bf16[24,2048]{1,0:T(8,128)(2,1)} fusion(bf16[192,2048]{1,0:T(8,128)(2,1)} %gather_fusion, f32[24,8]{1,0:T(8,128)S(1)} %copy.29, pred[24,8]{1,0:T(8,128)(4,1)S(1)} %get-tuple-element.5), kind=kLoop, calls=%fused_computation.15 | loop fusion | flops 1523712 | bytes 885696 | tf_op jit(solution)/shard_map/reduce_sum | solution.py:39
  (9 shorter events, 0.1 us)
Async XLA Ops:
  0.0 2.3 %copy-start = (bf16[24,2048]{1,0:T(8,128)(2,1)S(1)}, bf16[24,2048]{1,0:T(8,128)(2,1)}, u32[]{:S(2)}) copy-start(bf16[24,2048]{1,0:T(8,128)(2,1)} %param.5) | copy-start | bytes 294916
  117.5 4.4 %copy-start.1 = (f32[24,8]{0,1:T(8,128)S(1)}, f32[24,8]{0,1:T(8,128)}, u32[]{:S(2)}) copy-start(f32[24,8]{0,1:T(8,128)} %param.7) | copy-start | bytes 2308
  117.5 73.8 %all-to-all-start.1 = ((bf16[1,4,192,2048]{3,1,0,2:T(4,128)(2,1)}), bf16[1,4,192,2048]{3,1,0,2:T(4,128)(2,1)S(1)}, u32[]{:S(2)}, u32[]{:S(2)}) async-start(bf16[1,4,192,2048]{3,1,0,2:T(4,128)(2,1)} %copy.36), calls=%async_computation.1 | async-start | bytes 6291456 | tf_op jit(solution)/shard_map/all_to_all | solution.py:36
where the time goes:
time: 206 us; the launch traced here: 205 us
  blocking collectives  83.8 us (41%)
  waiting for transfers between devices  69.3 us (34%)
  local copies, waits for them, and re-layouts  25.9 us (13%)
  matrix products  17.8 us (9%)
  starting transfers between devices  4.25 us (2%)
  other arithmetic  4.01 us (2%)
    all_to_all x1, blocking collectives, local_layer(): recv_rows = lax.all_to_all(send_rows, 'ep', 0, 2, tiled=True)  83.8 us
    all_to_all x1, waiting for transfers between devices, local_layer(): back_rows = lax.all_to_all(expert_out, 'ep', 2, 0, tiled=True)  69.3 us
    dot_general x1, matrix products, local_layer(): jnp.einsum('ecf,efm->ecm', hidden, w_down, preferred_element_type=jnp.flo...  16.8 us
    reshape x2, local copies, waits for them, and re-layouts, local_layer(): send_rows = send_rows.reshape(group, local_experts, slot_cap, model_dim)  7.57 us
    reshape x1, local copies, waits for them, and re-layouts, local_layer(): expert_out.reshape(1, local_experts, group * slot_cap, model_dim)  6.02 us
    reshape x1, local copies, waits for them, and re-layouts, local_layer(): back_rows = back_rows.reshape(num_experts * slot_cap, model_dim)  4.71 us
    all_to_all x1, starting transfers between devices, local_layer(): back_rows = lax.all_to_all(expert_out, 'ep', 2, 0, tiled=True)  4.25 us
    all_to_all x1, local copies, waits for them, and re-layouts, local_layer(): back_rows = lax.all_to_all(expert_out, 'ep', 2, 0, tiled=True)  4.25 us
  transfers between devices with their start and end apart: 1, of which 1 were waited for; matrix products, arithmetic and copies ran while one was open for 0% of the time, Pallas kernels for 0%

commit v1 on v0

v1 whole, which is shorter than its diff:
```python
import functools

import jax
import jax.numpy as jnp
from jax import lax
from jax.experimental import pallas as pl
from jax.experimental.pallas import tpu as pltpu
from jax.sharding import PartitionSpec as P

MESH = pl.DeviceIdType.MESH
X_CHUNKS = 4
OUT_COLS = 256
UP_COLS = 512
LAG = 3
GATE_LANES = 128


def moe_kernel(group, x_ref, idx_ref, gate_ref, wu_hbm, wd_hbm, y_ref, xr, gr, xa, ga, wu, wd, hid, pb, pp, sb, rb,
               w_sem, ag_send, ag_recv, ex_send, ex_recv, rs_send, rs_recv):
    chips = group // 2
    half = chips // 2
    tok, dim = x_ref.shape
    experts, _, ff = wu.shape
    blocks = pb.shape[0]
    cols = pb.shape[-1]
    width = xr.shape[-1]
    chunks = xr.shape[0]
    rows = group * tok
    me = lax.axis_index('ep')
    chip, core = me // 2, me % 2

    def dev(c, k):
        return lax.rem(c + 2 * chips, chips) * 2 + k

    right, left, partner = dev(chip + 1, core), dev(chip - 1, core), dev(chip, 1 - core)

    def up_copy(e):
        return pltpu.make_async_copy(wu_hbm.at[e], wu.at[e], w_sem.at[0, e])

    def down_copy(e):
        return pltpu.make_async_copy(wd_hbm.at[e], wd.at[e], w_sem.at[1, e])

    for e in range(experts):
        up_copy(e).start()
    for e in range(experts):
        down_copy(e).start()

    barrier = pltpu.get_barrier_semaphore()
    for peer in (left, right, partner):
        pl.semaphore_signal(barrier, inc=1, device_id={'ep': peer}, device_id_type=MESH)

    lane = lax.broadcasted_iota(jnp.int32, (tok, GATE_LANES), 1)
    dense = jnp.zeros((tok, GATE_LANES), jnp.float32)
    for j in range(idx_ref.shape[1]):
        dense = dense + jnp.where(idx_ref[:, j:j + 1] == lane, gate_ref[:, j:j + 1], 0.0)
    gr[me] = dense
    for k in range(chunks):
        xr[k, me] = x_ref[:, k * width:(k + 1) * width]
    pl.semaphore_wait(barrier, 3)

    def slot(k, d):
        return gr.at[d] if k == chunks else xr.at[k, d]

    def source(k, d):
        if d is None:
            return gr.at[me] if k == chunks else x_ref.at[:, pl.ds(k * width, width)]
        return slot(k, d)

    def ag(k, d, peer, send):
        src = slot(k, me) if d is None else slot(k, d)
        owner = me if d is None else d
        return pltpu.make_async_remote_copy(
            src_ref=source(k, d), dst_ref=slot(k, owner), send_sem=ag_send.at[k, send], recv_sem=ag_recv.at[k, owner],
            device_id={'ep': peer}, device_id_type=MESH)

    sent = []

    def push(copy):
        copy.start()
        sent.append(copy)

    def far_right(k):
        return k % 2 == 0

    for k in range(chunks + 1):
        push(ag(k, None, right, 0))
        push(ag(k, None, left, half))
        push(ag(k, None, partner, 2 * half))
    for s in range(half):
        for k in range(chunks + 1):
            if s < half - 1 or far_right(k):
                d = dev(chip - 1 - s, core)
                ag(k, d, right, 0).wait_recv()
                if s + 1 < half - 1 or (s + 1 == half - 1 and far_right(k)):
                    push(ag(k, d, right, 1 + s))
                push(ag(k, d, partner, 2 * half + 1 + s))
            if s < half - 1 or not far_right(k):
                d = dev(chip + 1 + s, core)
                ag(k, d, left, half).wait_recv()
                if s + 1 < half - 1 or (s + 1 == half - 1 and not far_right(k)):
                    push(ag(k, d, left, half + 1 + s))
                push(ag(k, d, partner, 3 * half + 1 + s))
    for k in range(chunks + 1):
        def arrive(c, carry):
            ag(k, c * 2 + 1 - core, partner, 0).wait_recv()
            return carry
        lax.fori_loop(0, chips, arrive, 0)
    for k in range(chunks):
        def relayout(c, carry):
            pair = jnp.concatenate([xr[k, 2 * c], xr[k, 2 * c + 1]], axis=0)
            xa[pl.ds(pl.multiple_of(c * 2 * tok, 2 * tok), 2 * tok), k * width:(k + 1) * width] = pair
            return carry
        lax.fori_loop(0, chips, relayout, 0)

    up_blocks = ff // UP_COLS

    def up_step(i, carry):
        e, nb = i // up_blocks, i % up_blocks

        @pl.when(nb == 0)
        def _():
            up_copy(e).wait()
        span = pl.ds(pl.multiple_of(nb * UP_COLS, UP_COLS), UP_COLS)
        z = jnp.dot(xa[...], wu[e, :, span], preferred_element_type=jnp.float32)
        hid[e, :, span] = jax.nn.gelu(z, approximate=True).astype(jnp.bfloat16)
        return carry

    lax.fori_loop(0, experts * up_blocks, up_step, 0)

    all_lane = lax.broadcasted_iota(jnp.int32, (rows, GATE_LANES), 1)
    all_gates = gr[...].reshape(rows, GATE_LANES)
    for e in range(experts):
        one = jnp.sum(jnp.where(all_lane == me * experts + e, all_gates, 0.0), axis=1, keepdims=True)
        ga[e] = jnp.broadcast_to(one, (rows, GATE_LANES))
    for e in range(experts):
        down_copy(e).wait()

    def compute(b):
        span = pl.ds(pl.multiple_of(b * cols, cols), cols)
        total = None
        for e in range(experts):
            out = jnp.dot(hid[e], wd[e, :, span], preferred_element_type=jnp.float32)
            out = out.astype(jnp.bfloat16).astype(jnp.float32)
            gate = jnp.concatenate([ga[e]] * (cols // GATE_LANES), axis=1)
            term = jnp.where(gate > 0, gate * out, 0.0)
            total = term if total is None else total + term
        pb[b] = total.reshape(chips, 2, tok, cols)

    def exchange(b):
        return pltpu.make_async_remote_copy(
            src_ref=pb.at[b, :, 1 - core], dst_ref=pp.at[b], send_sem=ex_send.at[b], recv_sem=ex_recv.at[b],
            device_id={'ep': partner}, device_id_type=MESH)

    def local(b, c):
        c = lax.rem(c + 2 * chips, chips)
        return pb[b, c, core] + pp[b, c]

    def message(b, m, sign):
        return pltpu.make_async_remote_copy(
            src_ref=sb.at[b, m], dst_ref=rb.at[b, m], send_sem=rs_send.at[b, m], recv_sem=rs_recv.at[b, m],
            device_id={'ep': dev(chip + sign, core)}, device_id_type=MESH)

    def hop(b, j):
        sign = 1 - 2 * (b % 2)
        if j < half:
            value = local(b, chip + sign * (half - j))
            if j > 0:
                message(b, j - 1, sign).wait_recv()
                value = value + rb[b, j - 1]
            sb[b, j] = value
            message(b, j, sign).start()
        if j + 1 < half:
            m = half + j
            value = local(b, chip - sign * (half - j - 1))
            if j > 0:
                message(b, m - 1, -sign).wait_recv()
                value = value + rb[b, m - 1]
            sb[b, m] = value
            message(b, m, -sign).start()

    def finish(b):
        sign = 1 - 2 * (b % 2)
        value = local(b, chip)
        message(b, 2 * half - 2, -sign).wait_recv()
        value = value + rb[b, 2 * half - 2]
        message(b, half - 1, sign).wait_recv()
        value = value + rb[b, half - 1]
        y_ref[:, pl.ds(pl.multiple_of(b * cols, cols), cols)] = value.astype(y_ref.dtype)

    def at(t, delay, work):
        b = t - delay

        @pl.when((b >= 0) & (b < blocks))
        def _():
            work(b)

    def round_step(t, carry):
        def first(b):
            compute(b)
            exchange(b).start()
        at(t, 0, first)

        def begin(b):
            exchange(b).wait_recv()
            hop(b, 0)
        at(t, 1, begin)
        for j in range(1, half):
            at(t, 1 + j * LAG, lambda b, j=j: hop(b, j))
        at(t, 1 + half * LAG, finish)
        return carry

    lax.fori_loop(0, blocks + 1 + half * LAG, round_step, 0)

    for copy in sent:
        copy.wait_send()

    def drain(b, carry):
        sign = 1 - 2 * (b % 2)
        exchange(b).wait_send()
        for m in range(2 * half - 1):
            message(b, m, sign).wait_send()
        return carry

    lax.fori_loop(0, blocks, drain, 0)


def solution(mesh):
    group = mesh.shape['ep']
    token_spec = P(('dp', 'ep'), None)
    expert_spec = P('ep', None, None)

    def local_layer(x_loc, ids_loc, gates_loc, w_up, w_down):
        tok, dim = x_loc.shape
        experts, _, ff = w_up.shape
        chips = group // 2
        half = chips // 2
        blocks = dim // OUT_COLS
        width = dim // X_CHUNKS
        rows = group * tok
        vmem = pl.BlockSpec(memory_space=pltpu.VMEM)
        hbm = pl.BlockSpec(memory_space=pl.ANY)
        msgs = 2 * half - 1
        return pl.pallas_call(
            functools.partial(moe_kernel, group),
            out_shape=jax.ShapeDtypeStruct((tok, dim), jnp.bfloat16),
            in_specs=[vmem, vmem, vmem, hbm, hbm],
            out_specs=vmem,
            scratch_shapes=[
                pltpu.VMEM((X_CHUNKS, group, tok, width), jnp.bfloat16),
                pltpu.VMEM((group, tok, GATE_LANES), jnp.float32),
                pltpu.VMEM((rows, dim), jnp.bfloat16),
                pltpu.VMEM((experts, rows, GATE_LANES), jnp.float32),
                pltpu.VMEM((experts, dim, ff), jnp.bfloat16),
                pltpu.VMEM((experts, ff, dim), jnp.bfloat16),
                pltpu.VMEM((experts, rows, ff), jnp.bfloat16),
                pltpu.VMEM((blocks, chips, 2, tok, OUT_COLS), jnp.float32),
                pltpu.VMEM((blocks, chips, tok, OUT_COLS), jnp.float32),
                pltpu.VMEM((blocks, msgs, tok, OUT_COLS), jnp.float32),
                pltpu.VMEM((blocks, msgs, tok, OUT_COLS), jnp.float32),
                pltpu.SemaphoreType.DMA((2, experts)),
                pltpu.SemaphoreType.DMA((X_CHUNKS + 1, 4 * half + 1)),
                pltpu.SemaphoreType.DMA((X_CHUNKS + 1, group)),
                pltpu.SemaphoreType.DMA((blocks,)),
                pltpu.SemaphoreType.DMA((blocks,)),
                pltpu.SemaphoreType.DMA((blocks, msgs)),
                pltpu.SemaphoreType.DMA((blocks, msgs)),
            ],
            compiler_params=pltpu.CompilerParams(collective_id=0, has_side_effects=True, vmem_limit_bytes=62 * 1024 * 1024),
        )(x_loc, ids_loc, gates_loc, w_up, w_down)

    return jax.shard_map(local_layer, mesh=mesh, in_specs=(token_spec, token_spec, token_spec, expert_spec, expert_spec), out_specs=token_spec, check_vma=False)
```

time: 206 us -> 65.5 us (0.32)
  blocking collectives: 83.8 us -> 0 us
  waiting for transfers between devices: 69.3 us -> 0 us
  Pallas kernels: 0 us -> 60.9 us
  local copies, waits for them, and re-layouts: 25.9 us -> 4.25 us
  matrix products: 17.8 us -> 0 us
  starting transfers between devices: 4.25 us -> 0 us
  other arithmetic: 4.01 us -> 0 us
    all_to_all x1 -> x0, blocking collectives: 83.8 us -> none  [local_layer(): recv_rows = lax.all_to_all(send_rows, 'ep', 0, 2, tiled=True)]
    all_to_all x1 -> x0, waiting for transfers between devices: 69.3 us -> none  [local_layer(): back_rows = lax.all_to_all(expert_out, 'ep', 2, 0, tiled=True)]
    pallas_call x0 -> x1, Pallas kernels: none -> 60.9 us  [local_layer(): pl.pallas_call(functools.partial(moe_kernel, group), out_shape=jax.ShapeD...]
    reshape x5 -> x0, local copies, waits for them, and re-layouts: 18.4 us -> none  [the longest x2 7.57 us: local_layer(): send_rows = send_rows.reshape(group, local_experts, slot_cap, model_dim)]
    dot_general x2 -> x0, matrix products: 17.8 us -> none  [the longest x1 16.8 us: local_layer(): jnp.einsum('ecf,efm->ecm', hidden, w_down, preferred_element_type=jnp.flo...]
    all_to_all x1 -> x0, starting transfers between devices: 4.25 us -> none  [local_layer(): back_rows = lax.all_to_all(expert_out, 'ep', 2, 0, tiled=True)]
    all_to_all x1 -> x0, local copies, waits for them, and re-layouts: 4.25 us -> none  [local_layer(): back_rows = lax.all_to_all(expert_out, 'ep', 2, 0, tiled=True)]
    unnamed x6 -> x3, local copies, waits for them, and re-layouts: 0.88 us -> 4.25 us
  transfers between devices with their start and end apart: 1 -> 0, of which waited for: 1 -> 0; matrix products, arithmetic and copies ran while one was open for 0% -> 0% of each run, Pallas kernels for 0% -> 0%
where the time goes in v1:
time: 65.5 us; the launch traced here: 65.2 us
  Pallas kernels  60.9 us (93%)
  local copies, waits for them, and re-layouts  4.25 us (6%)
    pallas_call x1, Pallas kernels, local_layer(): pl.pallas_call(functools.partial(moe_kernel, group), out_shape=jax.ShapeD...  60.9 us
    unnamed x3, local copies, waits for them, and re-layouts  4.25 us

profile of v1, /device:TPU:21, one launch (start us, length us, event | category | flops | bytes accessed | tf_op | source)
XLA Modules:
  0.0 65.2 jit_solution(12755325876895577644)
XLA Ops:
  0.0 1.4 %copy.6.idx_ref = s32[24,8]{1,0:T(8,128)} copy(s32[24,8]{0,1:T(8,128)} %param.6) | data formatting | bytes 1536 | tf_op args[1]
  1.4 1.4 %copy.7.gate_ref = f32[24,8]{1,0:T(8,128)} copy(f32[24,8]{0,1:T(8,128)} %param.7) | data formatting | bytes 1536 | tf_op args[2]
  2.7 60.9 %shard_map.55 = bf16[24,2048]{1,0:T(8,128)(2,1)} custom-call(bf16[24,2048]{1,0:T(8,128)(2,1)} %x_ref.1, s32[24,8]{1,0:T(8,128)} %copy.6.idx_ref, f32[24,8]{1,0:T(8,128)} %copy.7.gate_ref, bf16[4,2048,1024]{2,1,0:T(8,128)(2,1)} %wu_hbm.1, bf16[4,1024,2048]{2,1,0:T(8,128)(2,1)} %wd_hbm.1), custom_call_target="tpu_custom_call" | custom-call | tf_op jit(solution)/shard_map/pallas_call | solution.py:243
  63.6 1.5 %copy.9 = bf16[24,2048]{1,0:T(8,128)(2,1)} copy(bf16[24,2048]{1,0:T(8,128)(2,1)} %shard_map.55) | data formatting | bytes 196608
